TPU v7x, 128 devices: a whole 4x4x4 slice. The times are simulated.
128 devices in a mesh: tm: 8 (over x_lo, y), space: 16 (over z, x_hi, core).
Axes of the slice: x: 4 (x_hi: 2, x_lo: 2; x = x_hi * 2 + x_lo), y: 4, z: 4, core: 2. Of those that a mesh axis runs over, the one named last changes fastest.
Arguments:
- thermal_field: float32 [512, 196608], P(('tm', 'space')), may hold values from 245 to 255
- seasonal_bucket: int32 [512], replicated, may hold values from 0 to 45, as said below
- season_of_record: int32 [512], replicated, may hold values from 0 to 7
Outputs:
- anomaly: float32 [512, 196608], P(('tm', 'space'))
Inputs may be any that keep to these rules, and one draw needn't show every extreme that they name: `seasonal_bucket`: every group holds at least one day whose year is below 6.
All inputs are finite; a program needn't handle non-finite values.
Results may differ from a plain program's by a relative error of at most 0.0003.
Values sent between devices are 32-bit elements; how exact they have to be, the bound alone decides.
A program may use at most 64 MiB of HBM per device.

v0:
```python
import jax
import jax.numpy as jnp
from jax import lax
from jax.sharding import PartitionSpec as P

GROUPS = 46
BASE_YEARS = 6


def shards(thermal_field, seasonal_bucket, season_of_record):
    group_ids = jnp.arange(GROUPS, dtype=jnp.int32)
    member = (seasonal_bucket[None, :] == group_ids[:, None]).astype(jnp.float32)
    reference_seasons = member * (season_of_record < BASE_YEARS).astype(jnp.float32)[None, :]
    counts = jnp.sum(reference_seasons, axis=1)
    column_blocks = lax.all_to_all(
        thermal_field, ("tm", "space"), split_axis=1, concat_axis=0, tiled=True
    )
    bucket_aggregates = jnp.dot(
        reference_seasons,
        column_blocks,
        precision=lax.Precision.HIGHEST,
        preferred_element_type=jnp.float32,
    )
    climate = bucket_aggregates / counts[:, None]
    chosen_records = jnp.dot(
        member.T, climate, precision=lax.Precision.HIGHEST, preferred_element_type=jnp.float32
    )
    result = lax.all_to_all(
        column_blocks - chosen_records, ("tm", "space"), split_axis=0, concat_axis=1, tiled=True
    )
    return result


def solution(mesh):
    placed = (P(("tm", "space"), None), P(), P())
    return jax.shard_map(
        shards, mesh=mesh, in_specs=placed, out_specs=P(("tm", "space"), None), check_vma=False
    )
```

profile of v0, /device:TPU:1, one launch (start us, length us, event | category | flops | bytes accessed | tf_op | source)
XLA Modules:
  0.0 114.0 jit_solution(7982285020159927800)
XLA Ops:
  0.0 0.0 copy-start.2
  0.0 0.0 copy-start.1
  0.0 11.5 %all-to-all-start = ((f32[4,128,1536]{2,0,1:T(4,128)}), f32[4,128,1536]{2,0,1:T(4,128)S(1)}, u32[]{:S(2)}, u32[]{:S(2)}) async-start(f32[4,128,1536]{2,0,1:T(4,128)} %bitcast.9), calls=%async_computation | async-start | bytes 6291456 | tf_op jit(solution)/shard_map/all_to_all | solution.py:15
  11.5 0.0 copy-done.2
  11.5 0.0 copy-done.1
  11.5 0.1 select_reduce_fusion
  11.6 41.5 %all-to-all-done = f32[4,128,1536]{2,0,1:T(4,128)S(1)} async-done(((f32[4,128,1536]{2,0,1:T(4,128)}), f32[4,128,1536]{2,0,1:T(4,128)S(1)}, u32[]{:S(2)}, u32[]{:S(2)}) %all-to-all-start) | async-done | bytes 3145760 | tf_op jit(solution)/shard_map/all_to_all | solution.py:15
  53.1 0.0 copy-start
  53.2 1.7 %copy-done = f32[4,128,1536]{2,0,1:T(4,128)} copy-done((f32[4,128,1536]{2,0,1:T(4,128)}, f32[4,128,1536]{2,0,1:T(4,128)S(1)}, u32[]{:S(2)}) %copy-start) | copy-done | bytes 3145752
  54.8 3.2 %all_to_all.31 = f32[512,1536]{1,0:T(8,128)S(1)} reshape(f32[128,4,1536]{2,1,0:T(4,128)} %bitcast.7) | data formatting | bytes 6291456 | tf_op jit(solution)/shard_map/all_to_all | solution.py:15
  58.0 2.0 %convolution_divide_fusion = f32[46,1536]{1,0:T(8,128)S(1)} fusion(f32[512,1536]{1,0:T(8,128)S(1)} %all_to_all.31, f32[46]{0:T(128)S(1)} %select_reduce_fusion, f32[512]{0:T(512)S(1)} %compare_convert_fusion, s32[512]{0:T(512)S(1)} %copy-done.1), kind=kOutput, calls=%fused_computation.1 | convolution fusion | flops 434228224 | bytes 3432632 | tf_op jit(solution)/shard_map/dot_general | solution.py:18
  60.0 3.1 %convolution_subtract_fusion = f32[512,1536]{1,0:T(8,128)} fusion(f32[512,1536]{1,0:T(8,128)S(1)} %all_to_all.31, f32[46,1536]{1,0:T(8,128)S(1)} %convolution_divide_fusion, s32[512]{0:T(512)S(1)} %copy-done.1), kind=kOutput, calls=%fused_computation | convolution fusion | flops 434920448 | bytes 6576128 | tf_op jit(solution)/shard_map/dot_general | solution.py:25
  63.1 3.1 %all_to_all.32 = f32[128,4,1536]{2,1,0:T(4,128)S(1)} reshape(f32[512,1536]{1,0:T(8,128)} %convolution_subtract_fusion) | data formatting | bytes 6291456 | tf_op jit(solution)/shard_map/all_to_all | solution.py:28
  66.2 46.1 %all_to_all.38 = f32[128,4,1536]{2,1,0:T(4,128)S(1)} all-to-all(f32[128,4,1536]{2,1,0:T(4,128)S(1)} %all_to_all.32), channel_id=1, replica_groups=mesh['tm'=8,'space'=16] {'tm','space'}, dimensions={0} | all-to-all | bytes 6291456 | tf_op jit(solution)/shard_map/all_to_all | solution.py:28
  112.3 1.7 %copy.9 = f32[4,196608]{1,0:T(4,128)} copy(f32[4,196608]{1,0:T(4,128)S(1)} %bitcast.8) | data formatting | bytes 6291456
  (1 shorter events, 0.0 us)
Async XLA Ops:
  0.0 11.5 %copy-start.2 = (s32[512]{0:T(512)S(1)}, s32[512]{0:T(512)}, u32[]{:S(2)}) copy-start(s32[512]{0:T(512)} %param.5) | copy-start | bytes 6148
  0.0 11.5 %copy-start.1 = (s32[512]{0:T(512)S(1)}, s32[512]{0:T(512)}, u32[]{:S(2)}) copy-start(s32[512]{0:T(512)} %param.4) | copy-start | bytes 6148
  0.0 53.1 %all-to-all-start = ((f32[4,128,1536]{2,0,1:T(4,128)}), f32[4,128,1536]{2,0,1:T(4,128)S(1)}, u32[]{:S(2)}, u32[]{:S(2)}) async-start(f32[4,128,1536]{2,0,1:T(4,128)} %bitcast.9), calls=%async_computation | async-start | bytes 6291456 | tf_op jit(solution)/shard_map/all_to_all | solution.py:15
  53.1 1.7 %copy-start = (f32[4,128,1536]{2,0,1:T(4,128)}, f32[4,128,1536]{2,0,1:T(4,128)S(1)}, u32[]{:S(2)}) copy-start(f32[4,128,1536]{2,0,1:T(4,128)S(1)} %all-to-all-done) | copy-start | bytes 9437188
where the time goes:
time: 114 us
  blocking collectives  46.1 us (40%)
  waiting for transfers between devices  41.5 us (36%)
  starting transfers between devices  11.5 us (10%)
  local copies, waits for them, and re-layouts  9.62 us (8%)
  matrix products  5.08 us (4%)
    all_to_all x1, blocking collectives, shards(): lax.all_to_all(column_blocks - chosen_records, ('tm', 'space'), split_axi...  46.1 us
    all_to_all x1, waiting for transfers between devices, shards(): lax.all_to_all(thermal_field, ('tm', 'space'), split_axis=1, concat_axis=...  41.5 us
    all_to_all x1, starting transfers between devices, shards(): lax.all_to_all(thermal_field, ('tm', 'space'), split_axis=1, concat_axis=...  11.5 us
    unnamed x7, local copies, waits for them, and re-layouts  3.34 us
    all_to_all x1, local copies, waits for them, and re-layouts, shards(): lax.all_to_all(thermal_field, ('tm', 'space'), split_axis=1, concat_axis=...  3.19 us
    dot_general x1, matrix products, shards(): jnp.dot(member.T, climate, precision=lax.Precision.HIGHEST, preferred_ele...  3.11 us
    all_to_all x1, local copies, waits for them, and re-layouts, shards(): lax.all_to_all(column_blocks - chosen_records, ('tm', 'space'), split_axi...  3.1 us
  transfers between devices with their start and end apart: 1, of which 1 were waited for; matrix products, arithmetic and copies ran while one was open for 0% of the time, Pallas kernels for 0%

commit v1 on v0

v1 whole, which is shorter than its diff:
```python
import functools

import jax
import jax.numpy as jnp
from jax import lax
from jax.experimental import pallas as pl
from jax.experimental.pallas import tpu as pltpu
from jax.sharding import PartitionSpec as P

GROUPS = 46
BASE_YEARS = 6
MESH = pl.DeviceIdType.MESH
F32, BF16 = jnp.float32, jnp.bfloat16

Q = 4
HALF = 48
ROWS = 2 * HALF
PART = ROWS // 4


def coordinates():
    tm, space = lax.axis_index("tm"), lax.axis_index("space")
    x = lax.rem(lax.div(space, 2), 2) * 2 + lax.div(tm, 4)
    return (x, lax.rem(tm, 4), lax.div(space, 4), lax.rem(space, 2))


def device(x, y, z, core):
    return (lax.rem(x, 2) * 4 + y, z * 4 + lax.div(x, 2) * 2 + core)


def peer(me, axis, step, core_step=0):
    at = list(me)
    at[axis] = lax.rem(me[axis] + step, 4)
    at[3] = lax.rem(me[3] + core_step, 2)
    return at


def split(v):
    high = v.astype(BF16)
    rest = v - high.astype(F32)
    middle = rest.astype(BF16)
    low = (rest - middle.astype(F32)).astype(BF16)
    return high, middle, low


def dot3(one_hot, v):
    high, middle, low = split(v)
    dot = functools.partial(jnp.dot, preferred_element_type=F32)
    return dot(one_hot, high) + (dot(one_hot, middle) + dot(one_hot, low))


def kernel(
    x_ref, bucket_row, year_row, bucket_hbm, year_hbm, out_ref,
    buf_a, buf_b, part, got, climate, buf_y, buf_z, member, base_t, counts,
    bucket, year, recv, sent, small,
):
    me = coordinates()
    tiles = x_ref.shape[0] // 3
    chunk = tiles // Q
    na, nb = chunk // 8, chunk // 32

    load_bucket = pltpu.make_async_copy(bucket_hbm, bucket, small.at[0])
    load_year = pltpu.make_async_copy(year_hbm, year, small.at[1])
    load_bucket.start()
    load_year.start()

    barrier = pltpu.get_barrier_semaphore()
    partners = 0
    for axis in range(3):
        for step in range(1, 4):
            for core in range(2):
                pl.semaphore_signal(barrier, inc=1, device_id=device(*peer(me, axis, step, core)), device_id_type=MESH)
                partners += 1
    pl.semaphore_signal(barrier, inc=1, device_id=device(*peer(me, 0, 0, 1)), device_id_type=MESH)
    pl.semaphore_wait(barrier, partners + 1)

    def remote(src, dst, stage, t, q, to):
        pltpu.make_async_remote_copy(
            src_ref=src, dst_ref=dst, send_sem=sent.at[stage], recv_sem=recv.at[stage, t, q],
            device_id=device(*to), device_id_type=MESH,
        ).start()

    def local(src, dst, stage, t, q):
        pltpu.make_async_copy(src, dst, recv.at[stage, t, q]).start()

    def arrive(ref, stage, t, q):
        pltpu.make_async_copy(ref, ref, recv.at[stage, t, q]).wait()

    def axes(t):
        return t, (t + 1) % 3, (t + 2) % 3

    order = ((1, 0), (3, 0), (2, 0), (1, 1), (3, 1), (2, 1), (0, 1))

    def send_a(q):
        for t in range(3):
            mine = me[t] * 2 + me[3]
            local(x_ref.at[pl.ds(t * tiles + q * chunk + mine * na, na)], buf_a.at[t, q, mine], 0, t, q)
        for step, core in order:
            for t in range(3):
                to = peer(me, t, step, core)
                mine, theirs = me[t] * 2 + me[3], to[t] * 2 + to[3]
                remote(x_ref.at[pl.ds(t * tiles + q * chunk + theirs * na, na)], buf_a.at[t, q, mine], 0, t, q, to)

    def send_b(q):
        for t in range(3):
            _, b, _ = axes(t)
            arrive(buf_a.at[t, q], 0, t, q)
            for step in (1, 3, 2):
                to = peer(me, b, step)
                remote(buf_a.at[t, q, :, pl.ds(to[b] * nb, nb)], buf_b.at[t, q, me[b]], 1, t, q, to)
            local(buf_a.at[t, q, :, pl.ds(me[b] * nb, nb)], buf_b.at[t, q, me[b]], 1, t, q)

    def days(t, q):
        return jnp.concatenate(
            [buf_b[t, q, :, :, n].reshape(256, 128) for n in range(nb)], axis=1
        )

    def send_c(q):
        for t in range(3):
            _, _, c = axes(t)
            arrive(buf_b.at[t, q], 1, t, q)
            sums = dot3(base_t[t], days(t, q))
            for j in range(4):
                for n in range(nb):
                    part[t, q, j, n] = sums[PART * j : PART * (j + 1), 128 * n : 128 * (n + 1)]
            for step in (1, 3, 2):
                to = peer(me, c, step)
                remote(part.at[t, q, to[c]], got.at[t, q, step - 1], 2, t, q, to)

    def send_back_c(q):
        for t in range(3):
            _, _, c = axes(t)
            arrive(got.at[t, q], 2, t, q)
            total = (part[t, q, me[c]] + got[t, q, 0]) + (got[t, q, 1] + got[t, q, 2])
            climate[t, q, me[c]] = total / counts[me[c]][None]
            for step in (1, 3, 2):
                to = peer(me, c, step)
                remote(climate.at[t, q, me[c]], climate.at[t, q, me[c]], 3, t, q, to)

    def send_back_b(q):
        for t in range(3):
            _, b, _ = axes(t)
            arrive(climate.at[t, q, pl.ds(0, 3)], 3, t, q)
            rows = jnp.concatenate(
                [climate[t, q, :, n].reshape(ROWS, 128) for n in range(nb)], axis=1
            )
            rows = jnp.concatenate([rows, jnp.zeros((128 - ROWS, 128 * nb), F32)], axis=0)
            chosen = dot3(member[t], rows)
            for n in range(nb):
                buf_y[t, q, :, :, n] = buf_b[t, q, :, :, n] - chosen[:, 128 * n : 128 * (n + 1)].reshape(4, 8, 8, 128)
            for step in (1, 3, 2):
                to = peer(me, b, step)
                remote(buf_y.at[t, q, to[b]], buf_z.at[t, q, :, pl.ds(me[b] * nb, nb)], 4, t, q, to)
            local(buf_y.at[t, q, me[b]], buf_z.at[t, q, :, pl.ds(me[b] * nb, nb)], 4, t, q)

    def send_back_a(q):
        for t in range(3):
            arrive(buf_z.at[t, q], 4, t, q)
            mine = me[t] * 2 + me[3]
            here = out_ref.at[pl.ds(t * tiles + q * chunk + mine * na, na)]
            for step, core in order:
                to = peer(me, t, step, core)
                remote(buf_z.at[t, q, to[t] * 2 + to[3]], here, 5, t, q, to)
            local(buf_z.at[t, q, mine], here, 5, t, q)

    def finish(q):
        for t in range(3):
            arrive(out_ref.at[pl.ds(t * tiles + q * chunk, chunk)], 5, t, q)

    def prepare():
        load_bucket.wait()
        load_year.wait()
        group = lax.broadcasted_iota(jnp.int32, (HALF, 128), 0)
        seen = jnp.zeros((HALF, 128), F32)
        for r in range(4):
            days_row = jnp.where(year_row[r : r + 1] < BASE_YEARS, bucket_row[r : r + 1], -1)
            seen = seen + jnp.where(days_row == group, 1.0, 0.0)
        number = jnp.maximum(jnp.sum(seen, axis=1, keepdims=True), 1.0)
        number = jnp.broadcast_to(number, (HALF, 128))
        for j in range(4):
            at = (j % 2) * PART
            counts[j] = number[at : at + PART]
        sub = lax.broadcasted_iota(jnp.int32, (8, 128), 0)
        lane = lax.broadcasted_iota(jnp.int32, (8, 128), 1)
        day, column = lax.rem(sub, 4), lane - lax.div(sub, 4) * HALF
        for t in range(3):
            a, b, c = axes(t)

            rows, base_rows = [], []
            for i in range(32):
                at = list(me)
                at[a], at[b], at[3] = (i // 2) % 4, i // 8, i % 2
                tm, space = device(*at)
                first = (tm * 16 + space) * 4
                every = [bucket[first + d] for d in range(4)]
                based = [jnp.where(year[first + d] < BASE_YEARS, every[d], -1000) for d in range(4)]
                pick = lambda v: jnp.where(day == 0, v[0], jnp.where(day == 1, v[1], jnp.where(day == 2, v[2], v[3])))
                rows.append(jnp.where(pick(every) == column, 1.0, 0.0))
                base_rows.append(jnp.where(pick(based) == column, 1.0, 0.0))
            member[t] = jnp.concatenate(rows, axis=0).astype(BF16)
            base_t[t] = jnp.concatenate(base_rows, axis=0).T[:ROWS].astype(BF16)

    stages = (send_a, send_b, send_c, send_back_c, send_back_b, send_back_a, finish)
    send_a(0)
    send_a(1)
    prepare()
    for step in range(1, Q + len(stages) - 1):
        for k in reversed(range(len(stages))):
            q = step - k if k else step + 1
            if 0 <= q < Q:
                stages[k](q)

    for stage, ref in ((0, buf_a), (1, buf_b), (4, buf_z), (5, buf_z)):
        for t in range(3):
            for q in range(Q):
                dims = 7 if stage in (0, 5) else 3
                if stage == 1:
                    piece = ref.at[t, q, pl.ds(0, 3)]
                elif stage == 4:
                    piece = buf_b.at[t, q, pl.ds(0, 3)]
                else:
                    piece = ref.at[t, q, pl.ds(0, dims)]
                pltpu.make_async_copy(piece, piece, sent.at[stage]).wait()
    for stage in (2, 3):
        pltpu.make_async_copy(got, got, sent.at[stage]).wait()


def shards(thermal_field, seasonal_bucket, season_of_record):
    days_here, cells = thermal_field.shape
    blocks = cells // 128
    x = thermal_field.reshape(days_here, blocks, 128).transpose(1, 0, 2)
    x = x.reshape(blocks // 2, 2 * days_here, 128)
    tiles = blocks // 2 // 3
    na, nb = tiles // Q // 8, tiles // Q // 32
    hbm, vmem = pl.BlockSpec(memory_space=pl.ANY), pl.BlockSpec(memory_space=pltpu.VMEM)
    out = pl.pallas_call(
        kernel,
        out_shape=jax.ShapeDtypeStruct(x.shape, F32),
        in_specs=[hbm, vmem, vmem, hbm, hbm],
        out_specs=hbm,
        scratch_shapes=[
            pltpu.VMEM((3, Q, 8, na, 8, 128), F32),
            pltpu.VMEM((3, Q, 4, 8, nb, 8, 128), F32),
            pltpu.VMEM((3, Q, 4, nb, PART, 128), F32),
            pltpu.VMEM((3, Q, 3, nb, PART, 128), F32),
            pltpu.VMEM((3, Q, 4, nb, PART, 128), F32),
            pltpu.VMEM((3, Q, 4, 8, nb, 8, 128), F32),
            pltpu.VMEM((3, Q, 8, na, 8, 128), F32),
            pltpu.VMEM((3, 256, 128), BF16),
            pltpu.VMEM((3, ROWS, 256), BF16),
            pltpu.VMEM((4, PART, 128), F32),
            pltpu.SMEM((512,), jnp.int32),
            pltpu.SMEM((512,), jnp.int32),
            pltpu.SemaphoreType.DMA((6, 3, Q)),
            pltpu.SemaphoreType.DMA((6,)),
            pltpu.SemaphoreType.DMA((2,)),
        ],
        compiler_params=pltpu.CompilerParams(
            collective_id=0, has_side_effects=True, vmem_limit_bytes=60 * 1024 * 1024
        ),
    )(
        x,
        seasonal_bucket.reshape(4, 128),
        season_of_record.reshape(4, 128),
        seasonal_bucket,
        season_of_record,
    )
    out = out.reshape(blocks, days_here, 128).transpose(1, 0, 2)
    return out.reshape(days_here, cells)


def solution(mesh):
    placed = (P(("tm", "space"), None), P(), P())
    return jax.shard_map(
        shards, mesh=mesh, in_specs=placed, out_specs=P(("tm", "space"), None), check_vma=False
    )
```

time: 114 us -> 72.9 us (0.64)
  Pallas kernels: 0 us -> 69.6 us
  blocking collectives: 46.1 us -> 0 us
  waiting for transfers between devices: 41.5 us -> 0 us
  starting transfers between devices: 11.5 us -> 0 us
  local copies, waits for them, and re-layouts: 9.62 us -> 3.18 us
  matrix products: 5.08 us -> 0 us
    pallas_call x0 -> x1, Pallas kernels: none -> 69.6 us  [shards(): pl.pallas_call(kernel, out_shape=jax.ShapeDtypeStruct(x.shape, F32), in_s...]
    all_to_all x1 -> x0, blocking collectives: 46.1 us -> none  [shards(): lax.all_to_all(column_blocks - chosen_records, ('tm', 'space'), split_axi...]
    all_to_all x1 -> x0, waiting for transfers between devices: 41.5 us -> none  [shards(): lax.all_to_all(thermal_field, ('tm', 'space'), split_axis=1, concat_axis=...]
    all_to_all x1 -> x0, starting transfers between devices: 11.5 us -> none  [shards(): lax.all_to_all(thermal_field, ('tm', 'space'), split_axis=1, concat_axis=...]
    all_to_all x2 -> x0, local copies, waits for them, and re-layouts: 6.28 us -> none  [the longest x1 3.19 us: shards(): lax.all_to_all(thermal_field, ('tm', 'space'), split_axis=1, concat_axis=...]
    dot_general x2 -> x0, matrix products: 5.08 us -> none  [the longest x1 3.11 us: shards(): jnp.dot(member.T, climate, precision=lax.Precision.HIGHEST, preferred_ele...]
    unnamed x7 -> x1, local copies, waits for them, and re-layouts: 3.34 us -> 3.18 us
  transfers between devices with their start and end apart: 1 -> 0, of which waited for: 1 -> 0; matrix products, arithmetic and copies ran while one was open for 0% -> 0% of each run, Pallas kernels for 0% -> 0%
where the time goes in v1:
time: 72.9 us; the launch traced here: 72.8 us
  Pallas kernels  69.6 us (95%)
  local copies, waits for them, and re-layouts  3.18 us (4%)
    pallas_call x1, Pallas kernels, shards(): pl.pallas_call(kernel, out_shape=jax.ShapeDtypeStruct(x.shape, F32), in_s...  69.6 us
    unnamed x1, local copies, waits for them, and re-layouts  3.18 us

profile of v1, /device:TPU:1, one launch (start us, length us, event | category | flops | bytes accessed | tf_op | source)
XLA Modules:
  0.0 72.8 jit_solution(7604188845360323867)
XLA Ops:
  0.0 69.6 %shard_map.37 = f32[768,8,128]{2,1,0:T(8,128)} custom-call(f32[768,8,128]{2,1,0:T(8,128)} %bitcast.13, s32[4,128]{1,0:T(4,128)} %bitcast.14, s32[4,128]{1,0:T(4,128)} %bitcast.15, s32[512]{0:T(512)} %bucket_hbm.1, s32[512]{0:T(512)} %year_hbm.1), custom_call_target="tpu_custom_call" | custom-call | tf_op jit(solution)/shard_map/pallas_call | solution.py:236
  69.6 3.2 %copy.7 = f32[4,196608]{1,0:T(4,128)} copy(f32[4,196608]{1,0:T(4,128)} %bitcast.12) | data formatting | bytes 6291456

commit v2 on v1

--- a/solution.py
+++ b/solution.py
@@ -200,15 +200,17 @@
             member[t] = jnp.concatenate(rows, axis=0).astype(BF16)
             base_t[t] = jnp.concatenate(base_rows, axis=0).T[:ROWS].astype(BF16)
 
-    stages = (send_a, send_b, send_c, send_back_c, send_back_b, send_back_a, finish)
+    stages = (send_a, send_b, send_c, send_back_c, send_back_b, send_back_a)
     send_a(0)
     send_a(1)
     prepare()
-    for step in range(1, Q + len(stages) - 1):
-        for k in reversed(range(len(stages))):
+    for step in range(1, Q + len(stages)):
+        for k in range(len(stages)):
             q = step - k if k else step + 1
             if 0 <= q < Q:
                 stages[k](q)
+    for q in range(Q):
+        finish(q)
 
     for stage, ref in ((0, buf_a), (1, buf_b), (4, buf_z), (5, buf_z)):
         for t in range(3):
@@ -235,7 +237,7 @@
     hbm, vmem = pl.BlockSpec(memory_space=pl.ANY), pl.BlockSpec(memory_space=pltpu.VMEM)
     out = pl.pallas_call(
         kernel,
-        out_shape=jax.ShapeDtypeStruct(x.shape, F32),
+        out_shape=pltpu.VMEM(x.shape, F32),
         in_specs=[hbm, vmem, vmem, hbm, hbm],
         out_specs=hbm,
         scratch_shapes=[
@@ -256,7 +258,7 @@
             pltpu.SemaphoreType.DMA((2,)),
         ],
         compiler_params=pltpu.CompilerParams(
-            collective_id=0, has_side_effects=True, vmem_limit_bytes=60 * 1024 * 1024
+            collective_id=0, has_side_effects=True, vmem_limit_bytes=63_880_000
         ),
     )(
         x,

time: 72.9 us -> 66.9 us (0.918)
  Pallas kernels: 69.6 us -> 65.1 us
  local copies, waits for them, and re-layouts: 3.18 us -> 1.67 us
    pallas_call x1, Pallas kernels: 69.6 us -> 65.1 us  [shards(): pl.pallas_call(kernel, out_shape=pltpu.VMEM(x.shape, F32), in_specs=[hbm,...]
    unnamed x1, local copies, waits for them, and re-layouts: 3.18 us -> 1.67 us
where the time goes in v2:
time: 66.9 us; the launch traced here: 66.7 us
  Pallas kernels  65.1 us (97%)
  local copies, waits for them, and re-layouts  1.67 us (2%)
    pallas_call x1, Pallas kernels, shards(): pl.pallas_call(kernel, out_shape=pltpu.VMEM(x.shape, F32), in_specs=[hbm,...  65.1 us
    unnamed x1, local copies, waits for them, and re-layouts  1.67 us

profile of v2, /device:TPU:1, one launch (start us, length us, event | category | flops | bytes accessed | tf_op | source)
XLA Modules:
  0.0 66.7 jit_solution(2264704957396149612)
XLA Ops:
  0.0 65.1 %shard_map.37 = f32[768,8,128]{2,1,0:T(8,128)S(1)} custom-call(f32[768,8,128]{2,1,0:T(8,128)} %bitcast.13, s32[4,128]{1,0:T(4,128)} %bitcast.14, s32[4,128]{1,0:T(4,128)} %bitcast.15, s32[512]{0:T(512)} %bucket_hbm.1, s32[512]{0:T(512)} %year_hbm.1), custom_call_target="tpu_custom_call" | custom-call | tf_op jit(solution)/shard_map/pallas_call | solution.py:238
  65.1 1.7 %copy.7 = f32[4,196608]{1,0:T(4,128)} copy(f32[4,196608]{1,0:T(4,128)S(1)} %bitcast.12) | data formatting | bytes 6291456

commit v3 on v2

v3 whole, which is shorter than its diff:
```python
import functools

import jax
import jax.numpy as jnp
from jax import lax
from jax.experimental import pallas as pl
from jax.experimental.pallas import tpu as pltpu
from jax.sharding import PartitionSpec as P

GROUPS = 46
BASE_YEARS = 6
MIDDLE = 250.0
MESH = pl.DeviceIdType.MESH
F32, BF16 = jnp.float32, jnp.bfloat16

Q = 4
HALF = 48
ROWS = 2 * HALF
PART = ROWS // 4


def coordinates():
    tm, space = lax.axis_index("tm"), lax.axis_index("space")
    x = lax.rem(lax.div(space, 2), 2) * 2 + lax.div(tm, 4)
    return (x, lax.rem(tm, 4), lax.div(space, 4), lax.rem(space, 2))


def device(x, y, z, core):
    return (lax.rem(x, 2) * 4 + y, z * 4 + lax.div(x, 2) * 2 + core)


def peer(me, axis, step, core_step=0):
    at = list(me)
    at[axis] = lax.rem(me[axis] + step, 4)
    at[3] = lax.rem(me[3] + core_step, 2)
    return at


def dot2(one_hot_twice, v):
    high = v.astype(BF16)
    low = (v - high.astype(F32)).astype(BF16)
    return jnp.dot(one_hot_twice, jnp.concatenate([high, low], axis=0), preferred_element_type=F32)


def halving(at, axis, h):
    m = at[axis]
    up = lax.rem(m + h, 2) == 0
    one, two = jnp.where(up, 1, 3), jnp.where(up, 3, 1)
    u = lax.rem(lax.div(m + 1 - h, 2), 2)
    v = lax.rem(m, 2) if h else lax.div(m, 2)
    return peer(at, axis, one), peer(at, axis, two), u, v


def kernel(
    x_ref, bucket_rows, year_rows, bucket_hbm, year_hbm, out_ref,
    buf_a, buf_b, part, kept, got_b, got_c, mean, got_e, buf_y, buf_z,
    member, base_t, counts, bucket_row, year_row, bucket, year, recv, sent, small,
):
    me = coordinates()
    tiles = x_ref.shape[0] // 3
    chunk = tiles // Q
    na = chunk // 8
    nh, nu, nv = na // 2, na // 4, na // 8

    loads = [
        pltpu.make_async_copy(src, dst, small.at[i])
        for i, (src, dst) in enumerate(
            ((bucket_hbm, bucket), (year_hbm, year), (bucket_rows, bucket_row), (year_rows, year_row))
        )
    ]
    for load in loads:
        load.start()

    barrier = pltpu.get_barrier_semaphore()
    partners = 0
    for axis in range(3):
        for step in range(1, 4):
            for core in range(2):
                pl.semaphore_signal(barrier, inc=1, device_id=device(*peer(me, axis, step, core)), device_id_type=MESH)
                partners += 1
    pl.semaphore_signal(barrier, inc=1, device_id=device(*peer(me, 0, 0, 1)), device_id_type=MESH)
    pl.semaphore_wait(barrier, partners + 1)

    def remote(src, dst, stage, t, q, h, to):
        pltpu.make_async_remote_copy(
            src_ref=src, dst_ref=dst, send_sem=sent.at[stage], recv_sem=recv.at[stage, t, q, h],
            device_id=device(*to), device_id_type=MESH,
        ).start()

    def local(src, dst, stage, t, q):
        pltpu.make_async_copy(src, dst, recv.at[stage, t, q, 0]).start()

    def arrive(ref, stage, t, q, h=0):
        pltpu.make_async_copy(ref, ref, recv.at[stage, t, q, h]).wait()

    def axes(t):
        return t, (t + 1) % 3, (t + 2) % 3

    order = ((1, 0), (3, 0), (2, 0), (1, 1), (3, 1), (2, 1), (0, 1))
    pairs = [(t, h) for t in range(3) for h in range(2)]

    def send_a(q):
        for t in range(3):
            mine = me[t] * 2 + me[3]
            local(x_ref.at[pl.ds(t * tiles + q * chunk + mine * na, na)], buf_a.at[t, q, mine], 0, t, q)
        for step, core in order:
            for t in range(3):
                to = peer(me, t, step, core)
                mine, theirs = me[t] * 2 + me[3], to[t] * 2 + to[3]
                remote(x_ref.at[pl.ds(t * tiles + q * chunk + theirs * na, na)], buf_a.at[t, q, mine], 0, t, q, 0, to)

    def send_b1(q):
        for t, h in pairs:
            if h == 0:
                arrive(buf_a.at[t, q], 0, t, q)
            one, _, u, _ = halving(me, axes(t)[1], h)
            remote(buf_a.at[t, q, :, pl.ds(h * nh + (1 - u) * nu, nu)], buf_b.at[t, q, h], 1, t, q, h, one)

    def send_b2(q):
        for t in range(3):
            sums = []
            for h in range(2):
                _, _, u, v = halving(me, axes(t)[1], h)
                arrive(buf_b.at[t, q, h], 1, t, q, h)
                columns = []
                for half in (1 - v, v):
                    for n in range(nv):
                        k = half * nv + n
                        mine = buf_a[t, q, :, h * nh + u * nu + k].reshape(64, 128)
                        theirs = buf_b[t, q, h, :, k].reshape(64, 128)
                        columns.append(jnp.concatenate([mine, theirs], axis=0))
                sums.append(dot2(base_t[t, h], jnp.concatenate(columns, axis=1) - MIDDLE))
            for h in range(2):
                for n in range(nv):
                    for j in range(4):
                        rows = slice(PART * j, PART * (j + 1))
                        part[t, q, h, j, n] = sums[h][rows, 128 * n : 128 * (n + 1)]
                        kept[t, q, j, h, n] = sums[h][rows, 128 * (nv + n) : 128 * (nv + n + 1)]
            for h in range(2):
                two = halving(me, axes(t)[1], h)[1]
                remote(part.at[t, q, h], got_b.at[t, q, h], 2, t, q, h, two)

    def send_c(q):
        for t in range(3):
            c = axes(t)[2]
            for h in range(2):
                arrive(got_b.at[t, q, h], 2, t, q, h)
                for j in range(4):
                    kept[t, q, j, h] += got_b[t, q, h, j]
            for step in (1, 3, 2):
                to = peer(me, c, step)
                remote(kept.at[t, q, to[c]], got_c.at[t, q, step - 1], 3, t, q, 0, to)

    def send_d(q):
        for t in range(3):
            c = axes(t)[2]
            arrive(got_c.at[t, q], 3, t, q)
            total = (kept[t, q, me[c]] + got_c[t, q, 0]) + (got_c[t, q, 1] + got_c[t, q, 2])
            mean[t, q, me[c]] = total / counts[me[c]][None, None]
            for step in (1, 3, 2):
                to = peer(me, c, step)
                remote(mean.at[t, q, me[c]], mean.at[t, q, me[c]], 4, t, q, 0, to)

    def send_e2(q):
        for t in range(3):
            arrive(mean.at[t, q, pl.ds(0, 3)], 4, t, q)
            for h in range(2):
                two = halving(me, axes(t)[1], h)[1]
                remote(mean.at[t, q, :, h], got_e.at[t, q, h], 5, t, q, h, two)

    def send_e1(q):
        for t in range(3):
            chosen = []
            for h in range(2):
                arrive(got_e.at[t, q, h], 5, t, q, h)
                rows = jnp.concatenate(
                    [mean[t, q, :, h, n].reshape(ROWS, 128) for n in range(nv)]
                    + [got_e[t, q, h, :, n].reshape(ROWS, 128) for n in range(nv)],
                    axis=1,
                )
                rows = jnp.concatenate([rows, jnp.zeros((128 - ROWS, 128 * nu), F32)], axis=0)
                chosen.append(dot2(member[t, h], rows))
            for h in range(2):
                one, _, u, v = halving(me, axes(t)[1], h)
                at = h * nh + u * nu
                for k in range(nu):
                    to = (v if k < nv else 1 - v) * nv + k % nv
                    column = chosen[h][64:, 128 * k : 128 * (k + 1)]
                    buf_y[t, q, h, :, to] = (buf_b[t, q, h, :, to] - MIDDLE) - column.reshape(8, 8, 128)
                remote(buf_y.at[t, q, h], buf_z.at[t, q, :, pl.ds(at, nu)], 6, t, q, h, one)
            for h in range(2):
                _, _, u, v = halving(me, axes(t)[1], h)
                at = h * nh + u * nu
                for k in range(nu):
                    to = at + (v if k < nv else 1 - v) * nv + k % nv
                    column = chosen[h][:64, 128 * k : 128 * (k + 1)]
                    buf_z[t, q, :, to] = (buf_a[t, q, :, to] - MIDDLE) - column.reshape(8, 8, 128)

    def send_f(q):
        for t in range(3):
            for h in range(2):
                arrive(buf_y.at[t, q, h], 6, t, q, h)
            mine = me[t] * 2 + me[3]
            here = out_ref.at[pl.ds(t * tiles + q * chunk + mine * na, na)]
            for step, core in order:
                to = peer(me, t, step, core)
                remote(buf_z.at[t, q, to[t] * 2 + to[3]], here, 7, t, q, 0, to)
            local(buf_z.at[t, q, mine], here, 7, t, q)

    def finish(q):
        for t in range(3):
            arrive(out_ref.at[pl.ds(t * tiles + q * chunk, chunk)], 7, t, q)

    def prepare():
        for load in loads:
            load.wait()
        group = lax.broadcasted_iota(jnp.int32, (HALF, 128), 0)
        seen = jnp.zeros((HALF, 128), F32)
        for r in range(4):
            days_row = jnp.where(year_row[r : r + 1] < BASE_YEARS, bucket_row[r : r + 1], -1)
            seen = seen + jnp.where(days_row == group, 1.0, 0.0)
        number = jnp.maximum(jnp.sum(seen, axis=1, keepdims=True), 1.0)
        number = jnp.broadcast_to(number, (HALF, 128))
        for j in range(4):
            at = (j % 2) * PART
            counts[j] = number[at : at + PART]
        sub = lax.broadcasted_iota(jnp.int32, (8, 128), 0)
        lane = lax.broadcasted_iota(jnp.int32, (8, 128), 1)
        day, column = lax.rem(sub, 4), lane - lax.div(sub, 4) * HALF

        def pick(v):
            chosen = jnp.where(day == 0, v[0], jnp.where(day == 1, v[1], jnp.where(day == 2, v[2], v[3])))
            return jnp.where(chosen == column, 1.0, 0.0)

        def line(at, a):
            every, based = [], []
            for i in range(8):
                who = list(at)
                who[a], who[3] = i // 2, i % 2
                tm, space = device(*who)
                first = (tm * 16 + space) * 4
                groups = [bucket[first + d] for d in range(4)]
                every.append(pick(groups))
                based.append(pick([jnp.where(year[first + d] < BASE_YEARS, groups[d], -1000) for d in range(4)]))
            return every, based

        for t in range(3):
            a, b, _ = axes(t)
            mine, mine_base = line(me, a)
            for h in range(2):
                theirs, theirs_base = line(halving(me, b, h)[0], a)
                every = jnp.concatenate(mine + theirs, axis=0).astype(BF16)
                based = jnp.concatenate(mine_base + theirs_base, axis=0).T[:ROWS].astype(BF16)
                member[t, h] = jnp.concatenate([every, every], axis=1)
                base_t[t, h] = jnp.concatenate([based, based], axis=1)

    stages = (send_a, send_b1, send_b2, send_c, send_d, send_e2, send_e1, send_f)
    stages[0](0)
    stages[0](1)
    stages[0](2)
    stages[0](3)
    prepare()
    stages[1](0)
    stages[1](1)
    stages[1](2)
    stages[1](3)
    stages[2](0)
    stages[2](1)
    stages[2](2)
    stages[2](3)
    stages[3](0)
    stages[3](1)
    stages[3](2)
    stages[3](3)
    stages[4](0)
    stages[4](1)
    stages[4](2)
    stages[4](3)
    stages[5](0)
    stages[5](1)
    stages[5](2)
    stages[5](3)
    stages[6](0)
    stages[6](1)
    stages[6](2)
    stages[6](3)
    stages[7](0)
    stages[7](1)
    stages[7](2)
    stages[7](3)
    for q in range(Q):
        finish(q)

    for stage, ref in ((0, buf_a), (7, buf_z)):
        for t in range(3):
            for q in range(Q):
                piece = ref.at[t, q, pl.ds(0, 7)]
                pltpu.make_async_copy(piece, piece, sent.at[stage]).wait()
    for stage, ref in ((1, buf_b), (2, got_b), (3, got_c), (4, got_c), (5, got_e), (6, buf_b)):
        pltpu.make_async_copy(ref, ref, sent.at[stage]).wait()


def shards(thermal_field, seasonal_bucket, season_of_record):
    days_here, cells = thermal_field.shape
    blocks = cells // 128
    x = thermal_field.reshape(days_here, blocks, 128).transpose(1, 0, 2)
    x = x.reshape(blocks // 2, 2 * days_here, 128)
    tiles = blocks // 2 // 3
    na, nv = tiles // Q // 8, tiles // Q // 64
    hbm = pl.BlockSpec(memory_space=pl.ANY)
    out = pl.pallas_call(
        kernel,
        out_shape=pltpu.VMEM(x.shape, F32),
        in_specs=[hbm] * 5,
        out_specs=hbm,
        scratch_shapes=[
            pltpu.VMEM((3, Q, 8, na, 8, 128), F32),
            pltpu.VMEM((3, Q, 2, 8, na // 4, 8, 128), F32),
            pltpu.VMEM((3, Q, 2, 4, nv, PART, 128), F32),
            pltpu.VMEM((3, Q, 4, 2, nv, PART, 128), F32),
            pltpu.VMEM((3, Q, 2, 4, nv, PART, 128), F32),
            pltpu.VMEM((3, Q, 3, 2, nv, PART, 128), F32),
            pltpu.VMEM((3, Q, 4, 2, nv, PART, 128), F32),
            pltpu.VMEM((3, Q, 2, 4, nv, PART, 128), F32),
            pltpu.VMEM((3, Q, 2, 8, na // 4, 8, 128), F32),
            pltpu.VMEM((3, Q, 8, na, 8, 128), F32),
            pltpu.VMEM((3, 2, 128, 256), BF16),
            pltpu.VMEM((3, 2, ROWS, 256), BF16),
            pltpu.VMEM((4, PART, 128), F32),
            pltpu.VMEM((4, 128), jnp.int32),
            pltpu.VMEM((4, 128), jnp.int32),
            pltpu.SMEM((512,), jnp.int32),
            pltpu.SMEM((512,), jnp.int32),
            pltpu.SemaphoreType.DMA((8, 3, Q, 2)),
            pltpu.SemaphoreType.DMA((8,)),
            pltpu.SemaphoreType.DMA((4,)),
        ],
        compiler_params=pltpu.CompilerParams(
            collective_id=0, has_side_effects=True, vmem_limit_bytes=63_880_000
        ),
    )(
        x,
        seasonal_bucket.reshape(4, 128),
        season_of_record.reshape(4, 128),
        seasonal_bucket,
        season_of_record,
    )
    out = out.reshape(blocks, days_here, 128).transpose(1, 0, 2)
    return out.reshape(days_here, cells)


def solution(mesh):
    placed = (P(("tm", "space"), None), P(), P())
    return jax.shard_map(
        shards, mesh=mesh, in_specs=placed, out_specs=P(("tm", "space"), None), check_vma=False
    )
```

time: 66.9 us -> 65.2 us (0.975)
  Pallas kernels: 65.1 us -> 63.4 us
    pallas_call x1, Pallas kernels: 65.1 us -> 63.4 us  [shards(): pl.pallas_call(kernel, out_shape=pltpu.VMEM(x.shape, F32), in_specs=[hbm]...]
where the time goes in v3:
time: 65.2 us; the launch traced here: 65.1 us
  Pallas kernels  63.4 us (97%)
  local copies, waits for them, and re-layouts  1.67 us (3%)
    pallas_call x1, Pallas kernels, shards(): pl.pallas_call(kernel, out_shape=pltpu.VMEM(x.shape, F32), in_specs=[hbm]...  63.4 us
    unnamed x1, local copies, waits for them, and re-layouts  1.67 us

profile of v3, /device:TPU:1, one launch (start us, length us, event | category | flops | bytes accessed | tf_op | source)
XLA Modules:
  0.0 65.1 jit_solution(7429487976873079427)
XLA Ops:
  0.0 63.4 %shard_map.37 = f32[768,8,128]{2,1,0:T(8,128)S(1)} custom-call(f32[768,8,128]{2,1,0:T(8,128)} %bitcast.13, s32[4,128]{1,0:T(4,128)} %bitcast.14, s32[4,128]{1,0:T(4,128)} %bitcast.15, s32[512]{0:T(512)} %bucket_hbm.1, s32[512]{0:T(512)} %year_hbm.1), custom_call_target="tpu_custom_call" | custom-call | tf_op jit(solution)/shard_map/pallas_call | solution.py:311
  63.4 1.7 %copy.7 = f32[4,196608]{1,0:T(4,128)} copy(f32[4,196608]{1,0:T(4,128)S(1)} %bitcast.12) | data formatting | bytes 6291456

commit v4 on v3

--- a/solution.py
+++ b/solution.py
@@ -17,6 +17,7 @@
 HALF = 48
 ROWS = 2 * HALF
 PART = ROWS // 4
+REAL = GROUPS // 2
 
 
 def coordinates():
@@ -97,6 +98,8 @@
         return t, (t + 1) % 3, (t + 2) % 3
 
     order = ((1, 0), (3, 0), (2, 0), (1, 1), (3, 1), (2, 1), (0, 1))
+    real = pl.ds(0, REAL)
+    row = lax.broadcasted_iota(jnp.int32, (4, PART, 128), 1)
     pairs = [(t, h) for t in range(3) for h in range(2)]
 
     def send_a(q):
@@ -138,44 +141,44 @@
                         kept[t, q, j, h, n] = sums[h][rows, 128 * (nv + n) : 128 * (nv + n + 1)]
             for h in range(2):
                 two = halving(me, axes(t)[1], h)[1]
-                remote(part.at[t, q, h], got_b.at[t, q, h], 2, t, q, h, two)
+                remote(part.at[t, q, h, :, :, real], got_b.at[t, q, h, :, :, real], 2, t, q, h, two)
 
     def send_c(q):
         for t in range(3):
             c = axes(t)[2]
             for h in range(2):
-                arrive(got_b.at[t, q, h], 2, t, q, h)
+                arrive(got_b.at[t, q, h, :, :, real], 2, t, q, h)
                 for j in range(4):
                     kept[t, q, j, h] += got_b[t, q, h, j]
             for step in (1, 3, 2):
                 to = peer(me, c, step)
-                remote(kept.at[t, q, to[c]], got_c.at[t, q, step - 1], 3, t, q, 0, to)
+                remote(kept.at[t, q, to[c], :, :, real], got_c.at[t, q, step - 1, :, :, real], 3, t, q, 0, to)
 
     def send_d(q):
         for t in range(3):
             c = axes(t)[2]
-            arrive(got_c.at[t, q], 3, t, q)
+            arrive(got_c.at[t, q, :, :, :, real], 3, t, q)
             total = (kept[t, q, me[c]] + got_c[t, q, 0]) + (got_c[t, q, 1] + got_c[t, q, 2])
             mean[t, q, me[c]] = total / counts[me[c]][None, None]
             for step in (1, 3, 2):
                 to = peer(me, c, step)
-                remote(mean.at[t, q, me[c]], mean.at[t, q, me[c]], 4, t, q, 0, to)
+                remote(mean.at[t, q, me[c], :, :, real], mean.at[t, q, me[c], :, :, real], 4, t, q, 0, to)
 
     def send_e2(q):
         for t in range(3):
-            arrive(mean.at[t, q, pl.ds(0, 3)], 4, t, q)
+            arrive(mean.at[t, q, pl.ds(0, 3), :, :, real], 4, t, q)
             for h in range(2):
                 two = halving(me, axes(t)[1], h)[1]
-                remote(mean.at[t, q, :, h], got_e.at[t, q, h], 5, t, q, h, two)
+                remote(mean.at[t, q, :, h, :, real], got_e.at[t, q, h, :, :, real], 5, t, q, h, two)
 
     def send_e1(q):
         for t in range(3):
             chosen = []
             for h in range(2):
-                arrive(got_e.at[t, q, h], 5, t, q, h)
+                arrive(got_e.at[t, q, h, :, :, real], 5, t, q, h)
                 rows = jnp.concatenate(
-                    [mean[t, q, :, h, n].reshape(ROWS, 128) for n in range(nv)]
-                    + [got_e[t, q, h, :, n].reshape(ROWS, 128) for n in range(nv)],
+                    [jnp.where(row < REAL, mean[t, q, :, h, n], 0.0).reshape(ROWS, 128) for n in range(nv)]
+                    + [jnp.where(row < REAL, got_e[t, q, h, :, n], 0.0).reshape(ROWS, 128) for n in range(nv)],
                     axis=1,
                 )
                 rows = jnp.concatenate([rows, jnp.zeros((128 - ROWS, 128 * nu), F32)], axis=0)
@@ -211,13 +214,16 @@
         for t in range(3):
             arrive(out_ref.at[pl.ds(t * tiles + q * chunk, chunk)], 7, t, q)
 
+    def place(group):
+        return group + jnp.where(group < REAL, 0, 1)
+
     def prepare():
         for load in loads:
             load.wait()
         group = lax.broadcasted_iota(jnp.int32, (HALF, 128), 0)
         seen = jnp.zeros((HALF, 128), F32)
         for r in range(4):
-            days_row = jnp.where(year_row[r : r + 1] < BASE_YEARS, bucket_row[r : r + 1], -1)
+            days_row = jnp.where(year_row[r : r + 1] < BASE_YEARS, place(bucket_row[r : r + 1]), -1)
             seen = seen + jnp.where(days_row == group, 1.0, 0.0)
         number = jnp.maximum(jnp.sum(seen, axis=1, keepdims=True), 1.0)
         number = jnp.broadcast_to(number, (HALF, 128))
@@ -239,7 +245,7 @@
                 who[a], who[3] = i // 2, i % 2
                 tm, space = device(*who)
                 first = (tm * 16 + space) * 4
-                groups = [bucket[first + d] for d in range(4)]
+                groups = [place(bucket[first + d]) for d in range(4)]
                 every.append(pick(groups))
                 based.append(pick([jnp.where(year[first + d] < BASE_YEARS, groups[d], -1000) for d in range(4)]))
             return every, based
@@ -296,7 +302,7 @@
             for q in range(Q):
                 piece = ref.at[t, q, pl.ds(0, 7)]
                 pltpu.make_async_copy(piece, piece, sent.at[stage]).wait()
-    for stage, ref in ((1, buf_b), (2, got_b), (3, got_c), (4, got_c), (5, got_e), (6, buf_b)):
+    for stage, ref in ((1, buf_b), (2, got_b.at[:, :, :, :, :, real]), (3, got_c.at[:, :, :, :, :, real]), (4, got_c.at[:, :, :, :, :, real]), (5, got_e.at[:, :, :, :, :, real]), (6, buf_b)):
         pltpu.make_async_copy(ref, ref, sent.at[stage]).wait()
 
 

time: 65.2 us -> 64.6 us (level)
  no operation moved by 1% of the time
where the time goes in v4:
time: 64.6 us; the launch traced here: 64.5 us
  Pallas kernels  62.9 us (97%)
  local copies, waits for them, and re-layouts  1.67 us (3%)
    pallas_call x1, Pallas kernels, shards(): pl.pallas_call(kernel, out_shape=pltpu.VMEM(x.shape, F32), in_specs=[hbm]...  62.9 us
    unnamed x1, local copies, waits for them, and re-layouts  1.67 us

profile of v4, /device:TPU:1, one launch (start us, length us, event | category | flops | bytes accessed | tf_op | source)
XLA Modules:
  0.0 64.5 jit_solution(346782591567128859)
XLA Ops:
  0.0 62.9 %shard_map.37 = f32[768,8,128]{2,1,0:T(8,128)S(1)} custom-call(f32[768,8,128]{2,1,0:T(8,128)} %bitcast.13, s32[4,128]{1,0:T(4,128)} %bitcast.14, s32[4,128]{1,0:T(4,128)} %bitcast.15, s32[512]{0:T(512)} %bucket_hbm.1, s32[512]{0:T(512)} %year_hbm.1), custom_call_target="tpu_custom_call" | custom-call | tf_op jit(solution)/shard_map/pallas_call | solution.py:317
  62.9 1.7 %copy.7 = f32[4,196608]{1,0:T(4,128)} copy(f32[4,196608]{1,0:T(4,128)S(1)} %bitcast.12) | data formatting | bytes 6291456

commit v5 on v4

--- a/solution.py
+++ b/solution.py
@@ -13,6 +13,7 @@
 MESH = pl.DeviceIdType.MESH
 F32, BF16 = jnp.float32, jnp.bfloat16
 
+TOGETHER = (0, 1, 2, 3, 4, 5, 6, 7)
 Q = 4
 HALF = 48
 ROWS = 2 * HALF
@@ -62,6 +63,7 @@
     chunk = tiles // Q
     na = chunk // 8
     nh, nu, nv = na // 2, na // 4, na // 8
+    real = pl.ds(0, REAL)
 
     loads = [
         pltpu.make_async_copy(src, dst, small.at[i])
@@ -82,23 +84,34 @@
     pl.semaphore_signal(barrier, inc=1, device_id=device(*peer(me, 0, 0, 1)), device_id_type=MESH)
     pl.semaphore_wait(barrier, partners + 1)
 
-    def remote(src, dst, stage, t, q, h, to):
+    def slot(stage, t, q):
+        at = sum(Q if k in TOGETHER else 3 * Q for k in range(stage))
+        return recv.at[at + q if stage in TOGETHER else at + 3 * q + t]
+
+    def remote(src, dst, stage, t, q, to):
         pltpu.make_async_remote_copy(
-            src_ref=src, dst_ref=dst, send_sem=sent.at[stage], recv_sem=recv.at[stage, t, q, h],
+            src_ref=src, dst_ref=dst, send_sem=sent.at[stage], recv_sem=slot(stage, t, q),
             device_id=device(*to), device_id_type=MESH,
         ).start()
 
     def local(src, dst, stage, t, q):
-        pltpu.make_async_copy(src, dst, recv.at[stage, t, q, 0]).start()
-
-    def arrive(ref, stage, t, q, h=0):
-        pltpu.make_async_copy(ref, ref, recv.at[stage, t, q, h]).wait()
+        pltpu.make_async_copy(src, dst, slot(stage, t, q)).start()
+
+    def arrive(stage, t, q):
+        if stage in TOGETHER and t > 0:
+            return
+        thirds = slice(None) if stage in TOGETHER else t
+        ref = (
+            buf_a.at[thirds, q], buf_b.at[thirds, q], got_b.at[thirds, q, :, :, :, real],
+            got_c.at[thirds, q, :, :, :, real], mean.at[thirds, q, pl.ds(0, 3), :, :, real],
+            got_e.at[thirds, q, :, :, :, real], buf_y.at[thirds, q], buf_z.at[thirds, q],
+        )[stage]
+        pltpu.make_async_copy(ref, ref, slot(stage, t, q)).wait()
 
     def axes(t):
         return t, (t + 1) % 3, (t + 2) % 3
 
     order = ((1, 0), (3, 0), (2, 0), (1, 1), (3, 1), (2, 1), (0, 1))
-    real = pl.ds(0, REAL)
     row = lax.broadcasted_iota(jnp.int32, (4, PART, 128), 1)
     pairs = [(t, h) for t in range(3) for h in range(2)]
 
@@ -110,21 +123,22 @@
             for t in range(3):
                 to = peer(me, t, step, core)
                 mine, theirs = me[t] * 2 + me[3], to[t] * 2 + to[3]
-                remote(x_ref.at[pl.ds(t * tiles + q * chunk + theirs * na, na)], buf_a.at[t, q, mine], 0, t, q, 0, to)
+                remote(x_ref.at[pl.ds(t * tiles + q * chunk + theirs * na, na)], buf_a.at[t, q, mine], 0, t, q, to)
 
     def send_b1(q):
         for t, h in pairs:
             if h == 0:
-                arrive(buf_a.at[t, q], 0, t, q)
+                arrive(0, t, q)
             one, _, u, _ = halving(me, axes(t)[1], h)
-            remote(buf_a.at[t, q, :, pl.ds(h * nh + (1 - u) * nu, nu)], buf_b.at[t, q, h], 1, t, q, h, one)
+            remote(buf_a.at[t, q, :, pl.ds(h * nh + (1 - u) * nu, nu)], buf_b.at[t, q, h], 1, t, q, one)
 
     def send_b2(q):
         for t in range(3):
             sums = []
             for h in range(2):
                 _, _, u, v = halving(me, axes(t)[1], h)
-                arrive(buf_b.at[t, q, h], 1, t, q, h)
+                if h == 0:
+                    arrive(1, t, q)
                 columns = []
                 for half in (1 - v, v):
                     for n in range(nv):
@@ -141,41 +155,42 @@
                         kept[t, q, j, h, n] = sums[h][rows, 128 * (nv + n) : 128 * (nv + n + 1)]
             for h in range(2):
                 two = halving(me, axes(t)[1], h)[1]
-                remote(part.at[t, q, h, :, :, real], got_b.at[t, q, h, :, :, real], 2, t, q, h, two)
+                remote(part.at[t, q, h, :, :, real], got_b.at[t, q, h, :, :, real], 2, t, q, two)
 
     def send_c(q):
         for t in range(3):
             c = axes(t)[2]
-            for h in range(2):
-                arrive(got_b.at[t, q, h, :, :, real], 2, t, q, h)
+            arrive(2, t, q)
+            for h in range(2):
                 for j in range(4):
                     kept[t, q, j, h] += got_b[t, q, h, j]
             for step in (1, 3, 2):
                 to = peer(me, c, step)
-                remote(kept.at[t, q, to[c], :, :, real], got_c.at[t, q, step - 1, :, :, real], 3, t, q, 0, to)
+                remote(kept.at[t, q, to[c], :, :, real], got_c.at[t, q, step - 1, :, :, real], 3, t, q, to)
 
     def send_d(q):
         for t in range(3):
             c = axes(t)[2]
-            arrive(got_c.at[t, q, :, :, :, real], 3, t, q)
+            arrive(3, t, q)
             total = (kept[t, q, me[c]] + got_c[t, q, 0]) + (got_c[t, q, 1] + got_c[t, q, 2])
             mean[t, q, me[c]] = total / counts[me[c]][None, None]
             for step in (1, 3, 2):
                 to = peer(me, c, step)
-                remote(mean.at[t, q, me[c], :, :, real], mean.at[t, q, me[c], :, :, real], 4, t, q, 0, to)
+                remote(mean.at[t, q, me[c], :, :, real], mean.at[t, q, me[c], :, :, real], 4, t, q, to)
 
     def send_e2(q):
         for t in range(3):
-            arrive(mean.at[t, q, pl.ds(0, 3), :, :, real], 4, t, q)
+            arrive(4, t, q)
             for h in range(2):
                 two = halving(me, axes(t)[1], h)[1]
-                remote(mean.at[t, q, :, h, :, real], got_e.at[t, q, h, :, :, real], 5, t, q, h, two)
+                remote(mean.at[t, q, :, h, :, real], got_e.at[t, q, h, :, :, real], 5, t, q, two)
 
     def send_e1(q):
         for t in range(3):
             chosen = []
             for h in range(2):
-                arrive(got_e.at[t, q, h, :, :, real], 5, t, q, h)
+                if h == 0:
+                    arrive(5, t, q)
                 rows = jnp.concatenate(
                     [jnp.where(row < REAL, mean[t, q, :, h, n], 0.0).reshape(ROWS, 128) for n in range(nv)]
                     + [jnp.where(row < REAL, got_e[t, q, h, :, n], 0.0).reshape(ROWS, 128) for n in range(nv)],
@@ -190,7 +205,7 @@
                     to = (v if k < nv else 1 - v) * nv + k % nv
                     column = chosen[h][64:, 128 * k : 128 * (k + 1)]
                     buf_y[t, q, h, :, to] = (buf_b[t, q, h, :, to] - MIDDLE) - column.reshape(8, 8, 128)
-                remote(buf_y.at[t, q, h], buf_z.at[t, q, :, pl.ds(at, nu)], 6, t, q, h, one)
+                remote(buf_y.at[t, q, h], buf_z.at[t, q, :, pl.ds(at, nu)], 6, t, q, one)
             for h in range(2):
                 _, _, u, v = halving(me, axes(t)[1], h)
                 at = h * nh + u * nu
@@ -199,20 +214,31 @@
                     column = chosen[h][:64, 128 * k : 128 * (k + 1)]
                     buf_z[t, q, :, to] = (buf_a[t, q, :, to] - MIDDLE) - column.reshape(8, 8, 128)
 
-    def send_f(q):
-        for t in range(3):
-            for h in range(2):
-                arrive(buf_y.at[t, q, h], 6, t, q, h)
+    def ranked(axis):
+        m = me[axis]
+        first = jnp.where(m == 0, 1, 0)
+        second = jnp.where(m == 0, 3, jnp.where(m == 2, 1, 2))
+        third = jnp.where(m == 0, 2, jnp.where(m == 3, 1, 3))
+        return first, second, third
+
+    def send_f(q, ranks):
+        for t in range(3):
             mine = me[t] * 2 + me[3]
             here = out_ref.at[pl.ds(t * tiles + q * chunk + mine * na, na)]
-            for step, core in order:
-                to = peer(me, t, step, core)
-                remote(buf_z.at[t, q, to[t] * 2 + to[3]], here, 7, t, q, 0, to)
-            local(buf_z.at[t, q, mine], here, 7, t, q)
+            if 0 in ranks:
+                arrive(6, t, q)
+                to = peer(me, t, 0, 1)
+                remote(buf_z.at[t, q, to[t] * 2 + to[3]], here, 7, t, q, to)
+                local(buf_z.at[t, q, mine], here, 7, t, q)
+            for rank in ranks:
+                for core in (1, 0):
+                    to = list(me)
+                    to[t], to[3] = ranked(t)[rank], core
+                    remote(buf_z.at[t, q, to[t] * 2 + core], here, 7, t, q, to)
 
     def finish(q):
         for t in range(3):
-            arrive(out_ref.at[pl.ds(t * tiles + q * chunk, chunk)], 7, t, q)
+            arrive(7, t, q)
 
     def place(group):
         return group + jnp.where(group < REAL, 0, 1)
@@ -290,10 +316,10 @@
     stages[6](1)
     stages[6](2)
     stages[6](3)
-    stages[7](0)
-    stages[7](1)
-    stages[7](2)
-    stages[7](3)
+    send_f(0, (0, 1, 2))
+    send_f(1, (0, 1, 2))
+    send_f(2, (0, 1, 2))
+    send_f(3, (0, 1, 2))
     for q in range(Q):
         finish(q)
 
@@ -337,7 +363,7 @@
             pltpu.VMEM((4, 128), jnp.int32),
             pltpu.SMEM((512,), jnp.int32),
             pltpu.SMEM((512,), jnp.int32),
-            pltpu.SemaphoreType.DMA((8, 3, Q, 2)),
+            pltpu.SemaphoreType.DMA((sum(Q if k in TOGETHER else 3 * Q for k in range(8)),)),
             pltpu.SemaphoreType.DMA((8,)),
             pltpu.SemaphoreType.DMA((4,)),
         ],

time: 64.6 us -> 62.9 us (0.974)
  Pallas kernels: 62.9 us -> 61.1 us
    pallas_call x1, Pallas kernels: 62.9 us -> 61.1 us  [shards(): pl.pallas_call(kernel, out_shape=pltpu.VMEM(x.shape, F32), in_specs=[hbm]...]
where the time goes in v5:
time: 62.9 us; the launch traced here: 62.8 us
  Pallas kernels  61.1 us (97%)
  local copies, waits for them, and re-layouts  1.67 us (3%)
    pallas_call x1, Pallas kernels, shards(): pl.pallas_call(kernel, out_shape=pltpu.VMEM(x.shape, F32), in_specs=[hbm]...  61.1 us
    unnamed x1, local copies, waits for them, and re-layouts  1.67 us

profile of v5, /device:TPU:1, one launch (start us, length us, event | category | flops | bytes accessed | tf_op | source)
XLA Modules:
  0.0 62.8 jit_solution(14679222061291711835)
XLA Ops:
  0.0 61.1 %shard_map.37 = f32[768,8,128]{2,1,0:T(8,128)S(1)} custom-call(f32[768,8,128]{2,1,0:T(8,128)} %bitcast.13, s32[4,128]{1,0:T(4,128)} %bitcast.14, s32[4,128]{1,0:T(4,128)} %bitcast.15, s32[512]{0:T(512)} %bucket_hbm.1, s32[512]{0:T(512)} %year_hbm.1), custom_call_target="tpu_custom_call" | custom-call | tf_op jit(solution)/shard_map/pallas_call | solution.py:343
  61.1 1.7 %copy.7 = f32[4,196608]{1,0:T(4,128)} copy(f32[4,196608]{1,0:T(4,128)S(1)} %bitcast.12) | data formatting | bytes 6291456

commit v6 on v4

--- a/solution.py
+++ b/solution.py
@@ -14,6 +14,7 @@
 F32, BF16 = jnp.float32, jnp.bfloat16
 
 Q = 4
+LAST = 7 * Q
 HALF = 48
 ROWS = 2 * HALF
 PART = ROWS // 4
@@ -62,6 +63,7 @@
     chunk = tiles // Q
     na = chunk // 8
     nh, nu, nv = na // 2, na // 4, na // 8
+    real = pl.ds(0, REAL)
 
     loads = [
         pltpu.make_async_copy(src, dst, small.at[i])
@@ -75,56 +77,59 @@
     barrier = pltpu.get_barrier_semaphore()
     partners = 0
     for axis in range(3):
-        for step in range(1, 4):
+        for step in (2, 1, 3):
             for core in range(2):
                 pl.semaphore_signal(barrier, inc=1, device_id=device(*peer(me, axis, step, core)), device_id_type=MESH)
                 partners += 1
     pl.semaphore_signal(barrier, inc=1, device_id=device(*peer(me, 0, 0, 1)), device_id_type=MESH)
     pl.semaphore_wait(barrier, partners + 1)
 
-    def remote(src, dst, stage, t, q, h, to):
+    def remote(src, dst, stage, q, to):
         pltpu.make_async_remote_copy(
-            src_ref=src, dst_ref=dst, send_sem=sent.at[stage], recv_sem=recv.at[stage, t, q, h],
+            src_ref=src, dst_ref=dst, send_sem=sent.at[stage], recv_sem=recv.at[min(Q * stage + q, LAST)],
             device_id=device(*to), device_id_type=MESH,
         ).start()
 
-    def local(src, dst, stage, t, q):
-        pltpu.make_async_copy(src, dst, recv.at[stage, t, q, 0]).start()
-
-    def arrive(ref, stage, t, q, h=0):
-        pltpu.make_async_copy(ref, ref, recv.at[stage, t, q, h]).wait()
+    def local(src, dst, stage, q):
+        pltpu.make_async_copy(src, dst, recv.at[min(Q * stage + q, LAST)]).start()
+
+    def arrive(stage, q):
+        ref = (
+            buf_a.at[:, q], buf_b.at[:, q], got_b.at[:, q, :, :, :, real],
+            got_c.at[:, q, :, :, :, real], mean.at[:, q, pl.ds(0, 3), :, :, real],
+            got_e.at[:, q, :, :, :, real], buf_y.at[:, q], buf_z,
+        )[stage]
+        pltpu.make_async_copy(ref, ref, recv.at[min(Q * stage + q, LAST)]).wait()
 
     def axes(t):
         return t, (t + 1) % 3, (t + 2) % 3
 
-    order = ((1, 0), (3, 0), (2, 0), (1, 1), (3, 1), (2, 1), (0, 1))
-    real = pl.ds(0, REAL)
+    order = ((2, 0), (2, 1), (1, 0), (3, 0), (1, 1), (3, 1), (0, 1))
     row = lax.broadcasted_iota(jnp.int32, (4, PART, 128), 1)
     pairs = [(t, h) for t in range(3) for h in range(2)]
 
     def send_a(q):
         for t in range(3):
             mine = me[t] * 2 + me[3]
-            local(x_ref.at[pl.ds(t * tiles + q * chunk + mine * na, na)], buf_a.at[t, q, mine], 0, t, q)
+            local(x_ref.at[pl.ds(t * tiles + q * chunk + mine * na, na)], buf_a.at[t, q, mine], 0, q)
         for step, core in order:
             for t in range(3):
                 to = peer(me, t, step, core)
                 mine, theirs = me[t] * 2 + me[3], to[t] * 2 + to[3]
-                remote(x_ref.at[pl.ds(t * tiles + q * chunk + theirs * na, na)], buf_a.at[t, q, mine], 0, t, q, 0, to)
+                remote(x_ref.at[pl.ds(t * tiles + q * chunk + theirs * na, na)], buf_a.at[t, q, mine], 0, q, to)
 
     def send_b1(q):
+        arrive(0, q)
         for t, h in pairs:
-            if h == 0:
-                arrive(buf_a.at[t, q], 0, t, q)
             one, _, u, _ = halving(me, axes(t)[1], h)
-            remote(buf_a.at[t, q, :, pl.ds(h * nh + (1 - u) * nu, nu)], buf_b.at[t, q, h], 1, t, q, h, one)
+            remote(buf_a.at[t, q, :, pl.ds(h * nh + (1 - u) * nu, nu)], buf_b.at[t, q, h], 1, q, one)
 
     def send_b2(q):
+        arrive(1, q)
         for t in range(3):
             sums = []
             for h in range(2):
                 _, _, u, v = halving(me, axes(t)[1], h)
-                arrive(buf_b.at[t, q, h], 1, t, q, h)
                 columns = []
                 for half in (1 - v, v):
                     for n in range(nv):
@@ -141,41 +146,41 @@
                         kept[t, q, j, h, n] = sums[h][rows, 128 * (nv + n) : 128 * (nv + n + 1)]
             for h in range(2):
                 two = halving(me, axes(t)[1], h)[1]
-                remote(part.at[t, q, h, :, :, real], got_b.at[t, q, h, :, :, real], 2, t, q, h, two)
+                remote(part.at[t, q, h, :, :, real], got_b.at[t, q, h, :, :, real], 2, q, two)
 
     def send_c(q):
+        arrive(2, q)
         for t in range(3):
             c = axes(t)[2]
             for h in range(2):
-                arrive(got_b.at[t, q, h, :, :, real], 2, t, q, h)
                 for j in range(4):
                     kept[t, q, j, h] += got_b[t, q, h, j]
-            for step in (1, 3, 2):
+            for step in (2, 1, 3):
                 to = peer(me, c, step)
-                remote(kept.at[t, q, to[c], :, :, real], got_c.at[t, q, step - 1, :, :, real], 3, t, q, 0, to)
+                remote(kept.at[t, q, to[c], :, :, real], got_c.at[t, q, step - 1, :, :, real], 3, q, to)
 
     def send_d(q):
+        arrive(3, q)
         for t in range(3):
             c = axes(t)[2]
-            arrive(got_c.at[t, q, :, :, :, real], 3, t, q)
             total = (kept[t, q, me[c]] + got_c[t, q, 0]) + (got_c[t, q, 1] + got_c[t, q, 2])
             mean[t, q, me[c]] = total / counts[me[c]][None, None]
-            for step in (1, 3, 2):
+            for step in (2, 1, 3):
                 to = peer(me, c, step)
-                remote(mean.at[t, q, me[c], :, :, real], mean.at[t, q, me[c], :, :, real], 4, t, q, 0, to)
+                remote(mean.at[t, q, me[c], :, :, real], mean.at[t, q, me[c], :, :, real], 4, q, to)
 
     def send_e2(q):
-        for t in range(3):
-            arrive(mean.at[t, q, pl.ds(0, 3), :, :, real], 4, t, q)
+        arrive(4, q)
+        for t in range(3):
             for h in range(2):
                 two = halving(me, axes(t)[1], h)[1]
-                remote(mean.at[t, q, :, h, :, real], got_e.at[t, q, h, :, :, real], 5, t, q, h, two)
+                remote(mean.at[t, q, :, h, :, real], got_e.at[t, q, h, :, :, real], 5, q, two)
 
     def send_e1(q):
+        arrive(5, q)
         for t in range(3):
             chosen = []
             for h in range(2):
-                arrive(got_e.at[t, q, h, :, :, real], 5, t, q, h)
                 rows = jnp.concatenate(
                     [jnp.where(row < REAL, mean[t, q, :, h, n], 0.0).reshape(ROWS, 128) for n in range(nv)]
                     + [jnp.where(row < REAL, got_e[t, q, h, :, n], 0.0).reshape(ROWS, 128) for n in range(nv)],
@@ -190,7 +195,7 @@
                     to = (v if k < nv else 1 - v) * nv + k % nv
                     column = chosen[h][64:, 128 * k : 128 * (k + 1)]
                     buf_y[t, q, h, :, to] = (buf_b[t, q, h, :, to] - MIDDLE) - column.reshape(8, 8, 128)
-                remote(buf_y.at[t, q, h], buf_z.at[t, q, :, pl.ds(at, nu)], 6, t, q, h, one)
+                remote(buf_y.at[t, q, h], buf_z.at[t, q, :, pl.ds(at, nu)], 6, q, one)
             for h in range(2):
                 _, _, u, v = halving(me, axes(t)[1], h)
                 at = h * nh + u * nu
@@ -200,19 +205,14 @@
                     buf_z[t, q, :, to] = (buf_a[t, q, :, to] - MIDDLE) - column.reshape(8, 8, 128)
 
     def send_f(q):
-        for t in range(3):
-            for h in range(2):
-                arrive(buf_y.at[t, q, h], 6, t, q, h)
+        arrive(6, q)
+        for t in range(3):
             mine = me[t] * 2 + me[3]
             here = out_ref.at[pl.ds(t * tiles + q * chunk + mine * na, na)]
             for step, core in order:
                 to = peer(me, t, step, core)
-                remote(buf_z.at[t, q, to[t] * 2 + to[3]], here, 7, t, q, 0, to)
-            local(buf_z.at[t, q, mine], here, 7, t, q)
-
-    def finish(q):
-        for t in range(3):
-            arrive(out_ref.at[pl.ds(t * tiles + q * chunk, chunk)], 7, t, q)
+                remote(buf_z.at[t, q, to[t] * 2 + to[3]], here, 7, q, to)
+            local(buf_z.at[t, q, mine], here, 7, q)
 
     def place(group):
         return group + jnp.where(group < REAL, 0, 1)
@@ -264,9 +264,9 @@
     stages[0](0)
     stages[0](1)
     stages[0](2)
-    stages[0](3)
     prepare()
     stages[1](0)
+    stages[0](3)
     stages[1](1)
     stages[1](2)
     stages[1](3)
@@ -294,15 +294,12 @@
     stages[7](1)
     stages[7](2)
     stages[7](3)
-    for q in range(Q):
-        finish(q)
-
-    for stage, ref in ((0, buf_a), (7, buf_z)):
-        for t in range(3):
-            for q in range(Q):
-                piece = ref.at[t, q, pl.ds(0, 7)]
-                pltpu.make_async_copy(piece, piece, sent.at[stage]).wait()
-    for stage, ref in ((1, buf_b), (2, got_b.at[:, :, :, :, :, real]), (3, got_c.at[:, :, :, :, :, real]), (4, got_c.at[:, :, :, :, :, real]), (5, got_e.at[:, :, :, :, :, real]), (6, buf_b)):
+    arrive(7, 0)
+
+    for stage, ref in (
+        (0, buf_a.at[:, :, pl.ds(0, 7)]), (1, buf_b), (2, got_b.at[:, :, :, :, :, real]), (3, got_c.at[:, :, :, :, :, real]),
+        (4, got_c.at[:, :, :, :, :, real]), (5, got_e.at[:, :, :, :, :, real]), (6, buf_b), (7, buf_z.at[:, :, pl.ds(0, 7)]),
+    ):
         pltpu.make_async_copy(ref, ref, sent.at[stage]).wait()
 
 
@@ -337,7 +334,7 @@
             pltpu.VMEM((4, 128), jnp.int32),
             pltpu.SMEM((512,), jnp.int32),
             pltpu.SMEM((512,), jnp.int32),
-            pltpu.SemaphoreType.DMA((8, 3, Q, 2)),
+            pltpu.SemaphoreType.DMA((LAST + 1,)),
             pltpu.SemaphoreType.DMA((8,)),
             pltpu.SemaphoreType.DMA((4,)),
         ],

time: 64.6 us -> 62.7 us (0.971)
  Pallas kernels: 62.9 us -> 60.9 us
    pallas_call x1, Pallas kernels: 62.9 us -> 60.9 us  [shards(): pl.pallas_call(kernel, out_shape=pltpu.VMEM(x.shape, F32), in_specs=[hbm]...]
where the time goes in v6:
time: 62.7 us; the launch traced here: 62.6 us
  Pallas kernels  60.9 us (97%)
  local copies, waits for them, and re-layouts  1.67 us (3%)
    pallas_call x1, Pallas kernels, shards(): pl.pallas_call(kernel, out_shape=pltpu.VMEM(x.shape, F32), in_specs=[hbm]...  60.9 us
    unnamed x1, local copies, waits for them, and re-layouts  1.67 us

profile of v6, /device:TPU:1, one launch (start us, length us, event | category | flops | bytes accessed | tf_op | source)
XLA Modules:
  0.0 62.6 jit_solution(2960668991328899413)
XLA Ops:
  0.0 60.9 %shard_map.37 = f32[768,8,128]{2,1,0:T(8,128)S(1)} custom-call(f32[768,8,128]{2,1,0:T(8,128)} %bitcast.13, s32[4,128]{1,0:T(4,128)} %bitcast.14, s32[4,128]{1,0:T(4,128)} %bitcast.15, s32[512]{0:T(512)} %bucket_hbm.1, s32[512]{0:T(512)} %year_hbm.1), custom_call_target="tpu_custom_call" | custom-call | tf_op jit(solution)/shard_map/pallas_call | solution.py:314
  60.9 1.7 %copy.7 = f32[4,196608]{1,0:T(4,128)} copy(f32[4,196608]{1,0:T(4,128)S(1)} %bitcast.12) | data formatting | bytes 6291456

commit v7 on v6

--- a/solution.py
+++ b/solution.py
@@ -38,10 +38,12 @@
     return at
 
 
-def dot2(one_hot_twice, v):
+def dot3(one_hot_thrice, v):
     high = v.astype(BF16)
-    low = (v - high.astype(F32)).astype(BF16)
-    return jnp.dot(one_hot_twice, jnp.concatenate([high, low], axis=0), preferred_element_type=F32)
+    rest = v - high.astype(F32)
+    middle = rest.astype(BF16)
+    low = (rest - middle.astype(F32)).astype(BF16)
+    return jnp.dot(one_hot_thrice, jnp.concatenate([high, middle, low], axis=0), preferred_element_type=F32)
 
 
 def halving(at, axis, h):
@@ -137,24 +139,25 @@
                         mine = buf_a[t, q, :, h * nh + u * nu + k].reshape(64, 128)
                         theirs = buf_b[t, q, h, :, k].reshape(64, 128)
                         columns.append(jnp.concatenate([mine, theirs], axis=0))
-                sums.append(dot2(base_t[t, h], jnp.concatenate(columns, axis=1) - MIDDLE))
+                sums.append(dot3(base_t[t, h], jnp.concatenate(columns, axis=1) - MIDDLE))
             for h in range(2):
                 for n in range(nv):
                     for j in range(4):
                         rows = slice(PART * j, PART * (j + 1))
                         part[t, q, h, j, n] = sums[h][rows, 128 * n : 128 * (n + 1)]
                         kept[t, q, j, h, n] = sums[h][rows, 128 * (nv + n) : 128 * (nv + n + 1)]
-            for h in range(2):
-                two = halving(me, axes(t)[1], h)[1]
-                remote(part.at[t, q, h, :, :, real], got_b.at[t, q, h, :, :, real], 2, q, two)
+        for t, h in pairs:
+            two = halving(me, axes(t)[1], h)[1]
+            remote(part.at[t, q, h, :, :, real], got_b.at[t, q, h, :, :, real], 2, q, two)
 
     def send_c(q):
         arrive(2, q)
         for t in range(3):
-            c = axes(t)[2]
             for h in range(2):
                 for j in range(4):
                     kept[t, q, j, h] += got_b[t, q, h, j]
+        for t in range(3):
+            c = axes(t)[2]
             for step in (2, 1, 3):
                 to = peer(me, c, step)
                 remote(kept.at[t, q, to[c], :, :, real], got_c.at[t, q, step - 1, :, :, real], 3, q, to)
@@ -165,6 +168,8 @@
             c = axes(t)[2]
             total = (kept[t, q, me[c]] + got_c[t, q, 0]) + (got_c[t, q, 1] + got_c[t, q, 2])
             mean[t, q, me[c]] = total / counts[me[c]][None, None]
+        for t in range(3):
+            c = axes(t)[2]
             for step in (2, 1, 3):
                 to = peer(me, c, step)
                 remote(mean.at[t, q, me[c], :, :, real], mean.at[t, q, me[c], :, :, real], 4, q, to)
@@ -187,15 +192,13 @@
                     axis=1,
                 )
                 rows = jnp.concatenate([rows, jnp.zeros((128 - ROWS, 128 * nu), F32)], axis=0)
-                chosen.append(dot2(member[t, h], rows))
-            for h in range(2):
-                one, _, u, v = halving(me, axes(t)[1], h)
-                at = h * nh + u * nu
+                chosen.append(dot3(member[t, h], rows))
+            for h in range(2):
+                v = halving(me, axes(t)[1], h)[3]
                 for k in range(nu):
                     to = (v if k < nv else 1 - v) * nv + k % nv
                     column = chosen[h][64:, 128 * k : 128 * (k + 1)]
                     buf_y[t, q, h, :, to] = (buf_b[t, q, h, :, to] - MIDDLE) - column.reshape(8, 8, 128)
-                remote(buf_y.at[t, q, h], buf_z.at[t, q, :, pl.ds(at, nu)], 6, q, one)
             for h in range(2):
                 _, _, u, v = halving(me, axes(t)[1], h)
                 at = h * nh + u * nu
@@ -203,6 +206,9 @@
                     to = at + (v if k < nv else 1 - v) * nv + k % nv
                     column = chosen[h][:64, 128 * k : 128 * (k + 1)]
                     buf_z[t, q, :, to] = (buf_a[t, q, :, to] - MIDDLE) - column.reshape(8, 8, 128)
+        for t, h in pairs:
+            one, _, u, _ = halving(me, axes(t)[1], h)
+            remote(buf_y.at[t, q, h], buf_z.at[t, q, :, pl.ds(h * nh + u * nu, nu)], 6, q, one)
 
     def send_f(q):
         arrive(6, q)
@@ -257,8 +263,8 @@
                 theirs, theirs_base = line(halving(me, b, h)[0], a)
                 every = jnp.concatenate(mine + theirs, axis=0).astype(BF16)
                 based = jnp.concatenate(mine_base + theirs_base, axis=0).T[:ROWS].astype(BF16)
-                member[t, h] = jnp.concatenate([every, every], axis=1)
-                base_t[t, h] = jnp.concatenate([based, based], axis=1)
+                member[t, h] = jnp.concatenate([every] * 3, axis=1)
+                base_t[t, h] = jnp.concatenate([based] * 3, axis=1)
 
     stages = (send_a, send_b1, send_b2, send_c, send_d, send_e2, send_e1, send_f)
     stages[0](0)
@@ -327,8 +333,8 @@
             pltpu.VMEM((3, Q, 2, 4, nv, PART, 128), F32),
             pltpu.VMEM((3, Q, 2, 8, na // 4, 8, 128), F32),
             pltpu.VMEM((3, Q, 8, na, 8, 128), F32),
-            pltpu.VMEM((3, 2, 128, 256), BF16),
-            pltpu.VMEM((3, 2, ROWS, 256), BF16),
+            pltpu.VMEM((3, 2, 128, 384), BF16),
+            pltpu.VMEM((3, 2, ROWS, 384), BF16),
             pltpu.VMEM((4, PART, 128), F32),
             pltpu.VMEM((4, 128), jnp.int32),
             pltpu.VMEM((4, 128), jnp.int32),

time: 62.7 us -> 62.6 us (level)
  no operation moved by 1% of the time
where the time goes in v7:
time: 62.6 us; the launch traced here: 62.5 us
  Pallas kernels  60.8 us (97%)
  local copies, waits for them, and re-layouts  1.67 us (3%)
    pallas_call x1, Pallas kernels, shards(): pl.pallas_call(kernel, out_shape=pltpu.VMEM(x.shape, F32), in_specs=[hbm]...  60.8 us
    unnamed x1, local copies, waits for them, and re-layouts  1.67 us

profile of v7, /device:TPU:1, one launch (start us, length us, event | category | flops | bytes accessed | tf_op | source)
XLA Modules:
  0.0 62.5 jit_solution(776214519873196184)
XLA Ops:
  0.0 60.8 %shard_map.37 = f32[768,8,128]{2,1,0:T(8,128)S(1)} custom-call(f32[768,8,128]{2,1,0:T(8,128)} %bitcast.13, s32[4,128]{1,0:T(4,128)} %bitcast.14, s32[4,128]{1,0:T(4,128)} %bitcast.15, s32[512]{0:T(512)} %bucket_hbm.1, s32[512]{0:T(512)} %year_hbm.1), custom_call_target="tpu_custom_call" | custom-call | tf_op jit(solution)/shard_map/pallas_call | solution.py:320
  60.8 1.7 %copy.7 = f32[4,196608]{1,0:T(4,128)} copy(f32[4,196608]{1,0:T(4,128)S(1)} %bitcast.12) | data formatting | bytes 6291456

commit v8 on v7

--- a/solution.py
+++ b/solution.py
@@ -88,7 +88,7 @@
 
     def remote(src, dst, stage, q, to):
         pltpu.make_async_remote_copy(
-            src_ref=src, dst_ref=dst, send_sem=sent.at[stage], recv_sem=recv.at[min(Q * stage + q, LAST)],
+            src_ref=src, dst_ref=dst, send_sem=sent.at[0], recv_sem=recv.at[min(Q * stage + q, LAST)],
             device_id=device(*to), device_id_type=MESH,
         ).start()
 
@@ -306,7 +306,7 @@
         (0, buf_a.at[:, :, pl.ds(0, 7)]), (1, buf_b), (2, got_b.at[:, :, :, :, :, real]), (3, got_c.at[:, :, :, :, :, real]),
         (4, got_c.at[:, :, :, :, :, real]), (5, got_e.at[:, :, :, :, :, real]), (6, buf_b), (7, buf_z.at[:, :, pl.ds(0, 7)]),
     ):
-        pltpu.make_async_copy(ref, ref, sent.at[stage]).wait()
+        pltpu.make_async_copy(ref, ref, sent.at[0]).wait()
 
 
 def shards(thermal_field, seasonal_bucket, season_of_record):
@@ -341,7 +341,7 @@
             pltpu.SMEM((512,), jnp.int32),
             pltpu.SMEM((512,), jnp.int32),
             pltpu.SemaphoreType.DMA((LAST + 1,)),
-            pltpu.SemaphoreType.DMA((8,)),
+            pltpu.SemaphoreType.DMA((1,)),
             pltpu.SemaphoreType.DMA((4,)),
         ],
         compiler_params=pltpu.CompilerParams(

time: 62.6 us -> 62.5 us (level)
  no operation moved by 1% of the time
where the time goes in v8:
time: 62.5 us; the launch traced here: 62.4 us
  Pallas kernels  60.7 us (97%)
  local copies, waits for them, and re-layouts  1.67 us (3%)
    pallas_call x1, Pallas kernels, shards(): pl.pallas_call(kernel, out_shape=pltpu.VMEM(x.shape, F32), in_specs=[hbm]...  60.7 us
    unnamed x1, local copies, waits for them, and re-layouts  1.67 us

profile of v8, /device:TPU:1, one launch (start us, length us, event | category | flops | bytes accessed | tf_op | source)
XLA Modules:
  0.0 62.4 jit_solution(9068331478536070824)
XLA Ops:
  0.0 60.7 %shard_map.37 = f32[768,8,128]{2,1,0:T(8,128)S(1)} custom-call(f32[768,8,128]{2,1,0:T(8,128)} %bitcast.13, s32[4,128]{1,0:T(4,128)} %bitcast.14, s32[4,128]{1,0:T(4,128)} %bitcast.15, s32[512]{0:T(512)} %bucket_hbm.1, s32[512]{0:T(512)} %year_hbm.1), custom_call_target="tpu_custom_call" | custom-call | tf_op jit(solution)/shard_map/pallas_call | solution.py:320
  60.7 1.7 %copy.7 = f32[4,196608]{1,0:T(4,128)} copy(f32[4,196608]{1,0:T(4,128)S(1)} %bitcast.12) | data formatting | bytes 6291456

commit v9 on v8

--- a/solution.py
+++ b/solution.py
@@ -111,14 +111,14 @@
     pairs = [(t, h) for t in range(3) for h in range(2)]
 
     def send_a(q):
-        for t in range(3):
-            mine = me[t] * 2 + me[3]
-            local(x_ref.at[pl.ds(t * tiles + q * chunk + mine * na, na)], buf_a.at[t, q, mine], 0, q)
         for step, core in order:
             for t in range(3):
                 to = peer(me, t, step, core)
                 mine, theirs = me[t] * 2 + me[3], to[t] * 2 + to[3]
                 remote(x_ref.at[pl.ds(t * tiles + q * chunk + theirs * na, na)], buf_a.at[t, q, mine], 0, q, to)
+        for t in range(3):
+            mine = me[t] * 2 + me[3]
+            local(x_ref.at[pl.ds(t * tiles + q * chunk + mine * na, na)], buf_a.at[t, q, mine], 0, q)
 
     def send_b1(q):
         arrive(0, q)

time: 62.5 us -> 62.5 us (level)
  no operation moved by 1% of the time
where the time goes in v9:
time: 62.5 us; the launch traced here: 62.4 us
  Pallas kernels  60.7 us (97%)
  local copies, waits for them, and re-layouts  1.67 us (3%)
    pallas_call x1, Pallas kernels, shards(): pl.pallas_call(kernel, out_shape=pltpu.VMEM(x.shape, F32), in_specs=[hbm]...  60.7 us
    unnamed x1, local copies, waits for them, and re-layouts  1.67 us

profile of v9, /device:TPU:1, one launch (start us, length us, event | category | flops | bytes accessed | tf_op | source)
XLA Modules:
  0.0 62.4 jit_solution(12053303058115192720)
XLA Ops:
  0.0 60.7 %shard_map.37 = f32[768,8,128]{2,1,0:T(8,128)S(1)} custom-call(f32[768,8,128]{2,1,0:T(8,128)} %bitcast.13, s32[4,128]{1,0:T(4,128)} %bitcast.14, s32[4,128]{1,0:T(4,128)} %bitcast.15, s32[512]{0:T(512)} %bucket_hbm.1, s32[512]{0:T(512)} %year_hbm.1), custom_call_target="tpu_custom_call" | custom-call | tf_op jit(solution)/shard_map/pallas_call | solution.py:320
  60.7 1.7 %copy.7 = f32[4,196608]{1,0:T(4,128)} copy(f32[4,196608]{1,0:T(4,128)S(1)} %bitcast.12) | data formatting | bytes 6291456
